TPU v7x, 256 devices: a whole 4x4x8 slice. The times are simulated.
256 devices in a mesh: req: 32 (over x, z), mdl: 8 (over y, core).
Axes of the slice: x: 4, y: 4, z: 8, core: 2. Of those that a mesh axis runs over, the one named last changes fastest.
Arguments:
- hidden_state: bfloat16 [1024, 2880], P('req'), may hold values from -6 to 6
- cached_length_list: int32 [1024], P('req'), may hold values from 1 to 2047, as said below
- page_table: int32 [1024, 16], P('req'), may hold values from 0 to 5631, as said below
- paged_cache_store: bfloat16 [5632, 128, 1024], P('req', None, 'mdl'), may hold values from -68 to 68, as said below
- attention_gain: float32 [2880], replicated, may hold values from 0.5 to 1.5
- qkv_weight: bfloat16 [2880, 5120], P('req', 'mdl'), may hold values from -0.109375 to 0.109375
- qkv_bias: float32 [5120], P('mdl'), may hold values from -3 to 3
- sink_logit_values: float32 [64], P('mdl'), may hold values from -1 to 4
- output_weight: bfloat16 [4096, 2880], P('mdl', 'req'), may hold values from -0.25 to 0.25
- output_bias: float32 [2880], replicated, may hold values from -3 to 3
- expert_gain: float32 [2880], replicated, may hold values from 0.5 to 1.5
- router_weight: bfloat16 [2880, 32], replicated, may hold values from -0.109375 to 0.109375
- router_bias: float32 [32], replicated, may hold values from -4 to 4
- expert_routes: int32 [1024, 4], P('req'), may hold values from 0 to 31, all different within a row; in each aligned block of 32 rows (0 to 31, 32 to 63, ...) at most 8 rows name the same one
- expand_weight: bfloat16 [32, 2880, 5760], P('req', None, 'mdl'), may hold values from -0.109375 to 0.109375
- expand_bias: float32 [32, 5760], P('req', 'mdl'), may hold values from -10 to 10
- reduce_weight: bfloat16 [32, 2880, 2880], P('req', 'mdl'), may hold values from -0.109375 to 0.109375
- reduce_bias: float32 [32, 2880], replicated, may hold values from -3 to 3
Outputs:
- layer_output: bfloat16 [1024, 2880], P('req', 'mdl')
Inputs may be any that keep to these rules, and one draw needn't show every extreme that they name: `cached_length_list`: requests r and r + 1 within a block of 32 requests share an owner; about one request in eight holds between 1536 and 2047 cached positions, at most 8 of each owner's 32, and the others at most 256; some owner, and the last owner, hold exactly 8 long ones. `page_table`: the entries of request r name pages of its owner's block, pages r // 32 * 176 to that plus 176 - 1; the pages that hold cached positions differ between requests; entries past a request's last used page are to be ignored. `paged_cache_store`: keys are stored rotated at their own positions. `expert_routes`: each token names 4 different experts; of the rows of one index of req no expert is named by more than 8.
All inputs are finite; a program needn't handle non-finite values.
Results may differ from a plain program's by a relative error of at most 0.024.
Values may be sent and summed in bfloat16 or wider, within the bound.
A program may use at most 192 MiB of HBM per device.

v0:
```python
import math
import jax
import jax.numpy as jnp
from jax import lax
from jax.sharding import PartitionSpec as P

HEAD_SIZE = 64
PAGE_POSITIONS = 128
SHORT_MAX = 256
QUERY_PER_KEY = 8
SHORT_PAGES = 2
norm_epsilon = 1e-05
rope_theta = 150000.0
swiglu_limit = 7.0
swiglu_alpha = 1.702


def normalize(row_values, gain):
    value_rows = row_values.astype(jnp.float32)
    mean_square = jnp.mean(value_rows * value_rows, axis=-1, keepdims=True)
    return value_rows * lax.rsqrt(mean_square + norm_epsilon) * gain


def apply_rotation(value_rows, positions):
    half_width = value_rows.shape[-1] // 2
    exponent = jnp.arange(half_width, dtype=jnp.float32) * (2.0 / value_rows.shape[-1])
    frequency = jnp.power(rope_theta, -exponent)
    angles = positions.astype(jnp.float32)[:, None] * frequency[None, :]
    cosine = jnp.cos(angles)[:, None, :]
    sine_part = jnp.sin(angles)[:, None, :]
    first_half = value_rows[..., :half_width]
    second_half = value_rows[..., half_width:]
    return jnp.concatenate(
        [
            first_half * cosine - second_half * sine_part,
            second_half * cosine + first_half * sine_part,
        ],
        axis=-1,
    )


def head_identity(kv_heads):
    return (jnp.arange(kv_heads)[:, None] == jnp.arange(kv_heads)[None, :]).astype(jnp.float32)


def spread_queries(query_rows):
    row_count, kv_heads, group_size, head_width = query_rows.shape
    key_slot = (jnp.arange(2) == 0).astype(jnp.float32)
    turned = jnp.swapaxes(query_rows, 2, 3).astype(jnp.float32)
    spread = jnp.einsum("rhdg,kh,s->rksdhg", turned, head_identity(kv_heads), key_slot)
    return spread.astype(jnp.bfloat16).reshape(
        row_count, kv_heads * 2 * head_width, kv_heads * group_size
    )


def part_scores(query_block, table, first_position, lengths, cache_page_store, head_width):
    row_count = query_block.shape[0]
    cached_entries = cache_page_store[table].reshape(row_count, -1, cache_page_store.shape[-1])
    score_scale = 1.0 / math.sqrt(head_width)
    scores = (
        jnp.einsum("rlc,rcq->rql", cached_entries, query_block, preferred_element_type=jnp.float32)
        * score_scale
    )
    positions = first_position + jnp.arange(scores.shape[-1])
    is_live = positions[None, :] < lengths[:, None]
    scores = jnp.where(is_live[:, None, :], scores, -jnp.inf)
    return (cached_entries, scores)


def attend_cache(
    query_rows, new_keys, new_values, lengths, local_table, cache_page_store, sink_logits
):
    row_count, kv_heads, group_size, head_width = query_rows.shape
    score_scale = 1.0 / math.sqrt(head_width)
    query_block = spread_queries(query_rows)
    short_cached, short_scores = part_scores(
        query_block, local_table[:, :SHORT_PAGES], 0, lengths, cache_page_store, head_width
    )
    long_count = row_count // 4
    is_long = lengths > SHORT_MAX
    long_rows = jnp.nonzero(is_long, size=long_count, fill_value=0)[0].astype(jnp.int32)
    long_valid = jnp.arange(long_count) < jnp.sum(is_long.astype(jnp.int32))
    long_lengths = jnp.where(long_valid, lengths[long_rows], 0)
    long_cached, long_scores = part_scores(
        query_block[long_rows],
        local_table[long_rows, SHORT_PAGES:],
        SHORT_PAGES * PAGE_POSITIONS,
        long_lengths,
        cache_page_store,
        head_width,
    )
    own_score = (
        jnp.einsum(
            "rhgd,rhd->rhg", query_rows, new_keys, preferred_element_type=jnp.float32
        ).reshape(row_count, -1)
        * score_scale
    )
    largest = jnp.maximum(jnp.maximum(jnp.max(short_scores, axis=-1), own_score), sink_logits[None])
    largest = largest.at[long_rows].max(jnp.max(long_scores, axis=-1))
    long_largest = largest[long_rows]
    short_weight = jnp.exp(short_scores - largest[..., None])
    long_weight = jnp.exp(long_scores - long_largest[..., None])
    own_weight = jnp.exp(own_score - largest)
    denominator = jnp.sum(short_weight, axis=-1) + own_weight + jnp.exp(sink_logits[None] - largest)
    denominator = denominator.at[long_rows].add(jnp.sum(long_weight, axis=-1))
    long_denominator = denominator[long_rows]
    short_share = (short_weight / denominator[..., None]).astype(jnp.bfloat16)
    long_share = (long_weight / long_denominator[..., None]).astype(jnp.bfloat16)
    own_share = (own_weight / denominator).astype(jnp.bfloat16)
    wide_mixture = jnp.einsum(
        "rql,rlc->rqc", short_share, short_cached, preferred_element_type=jnp.float32
    )
    long_mixture = jnp.einsum(
        "rql,rlc->rqc", long_share, long_cached, preferred_element_type=jnp.float32
    )
    wide_mixture = wide_mixture.at[long_rows].add(long_mixture)
    wide_mixture = wide_mixture.reshape(row_count, kv_heads, group_size, kv_heads, 2, head_width)
    value_slot = (jnp.arange(2) == 1).astype(jnp.float32)
    mixture = jnp.einsum("rhgksd,hk,s->rhgd", wide_mixture, head_identity(kv_heads), value_slot)
    own_part = own_share.astype(jnp.float32).reshape(row_count, kv_heads, group_size)
    mixture = mixture + own_part[..., None] * new_values.astype(jnp.float32)[:, :, None, :]
    return mixture.astype(jnp.bfloat16).reshape(row_count, -1)


def expert_block(received, expand_local, expand_local_bias, reduce_local):
    sources, item_count, model_width = received.shape
    flattened = received.reshape(sources * item_count, model_width)
    pre_activation = (
        jnp.dot(flattened, expand_local, preferred_element_type=jnp.float32) + expand_local_bias
    )
    gate_part = jnp.minimum(pre_activation[:, 0::2], swiglu_limit)
    up_part = jnp.clip(pre_activation[:, 1::2], -swiglu_limit, swiglu_limit)
    activation = (gate_part * jax.nn.sigmoid(swiglu_alpha * gate_part) * (up_part + 1.0)).astype(
        jnp.bfloat16
    )
    return jnp.dot(activation, reduce_local, preferred_element_type=jnp.float32).reshape(
        sources, item_count, -1
    )


def shards(
    hidden_state,
    cached_length_list,
    page_table,
    paged_cache_store,
    attention_gain,
    qkv_weight,
    qkv_bias,
    sink_logit_values,
    output_weight,
    output_bias,
    expert_gain,
    router_weight,
    router_bias,
    expert_routes,
    expand_weight,
    expand_bias,
    reduce_weight,
    reduce_bias,
):
    rows_here, model_width = hidden_state.shape
    normed = normalize(hidden_state, attention_gain).astype(jnp.bfloat16)
    qkv_full, output_full = (
        lax.all_gather(qkv_weight, "req", axis=0, tiled=True),
        lax.all_gather(output_weight, "req", axis=1, tiled=True),
    )
    projected_rows = jnp.dot(normed, qkv_full, preferred_element_type=jnp.float32)
    projected_rows = (projected_rows + qkv_bias).reshape(
        rows_here, -1, QUERY_PER_KEY + 2, HEAD_SIZE
    )
    kv_heads = projected_rows.shape[1]
    query_rows = (
        apply_rotation(
            projected_rows[:, :, :QUERY_PER_KEY].reshape(
                rows_here, kv_heads * QUERY_PER_KEY, HEAD_SIZE
            ),
            cached_length_list,
        )
        .astype(jnp.bfloat16)
        .reshape(rows_here, kv_heads, QUERY_PER_KEY, HEAD_SIZE)
    )
    new_keys = apply_rotation(projected_rows[:, :, QUERY_PER_KEY], cached_length_list).astype(
        jnp.bfloat16
    )
    new_values = projected_rows[:, :, QUERY_PER_KEY + 1].astype(jnp.bfloat16)
    local_table = page_table - lax.axis_index("req") * paged_cache_store.shape[0]
    attended = attend_cache(
        query_rows,
        new_keys,
        new_values,
        cached_length_list,
        local_table,
        paged_cache_store,
        sink_logit_values,
    )
    partial_value = jnp.dot(attended, output_full, preferred_element_type=jnp.float32)
    head_total = lax.psum(partial_value.astype(jnp.bfloat16), "mdl").astype(jnp.float32)
    residual = (hidden_state.astype(jnp.float32) + head_total + output_bias).astype(jnp.bfloat16)
    expert_input = normalize(residual, expert_gain).astype(jnp.bfloat16)
    logits = jnp.dot(expert_input, router_weight, preferred_element_type=jnp.float32) + router_bias
    experts = router_weight.shape[1]
    route_count = expert_routes.shape[1]
    one_hot = expert_routes[:, :, None] == jnp.arange(experts)[None, None, :]
    chosen = jnp.sum(jnp.where(one_hot, logits[:, None, :], 0.0), axis=-1)
    gate_weights = jax.nn.softmax(chosen, axis=-1)
    capacity = max(2, 2 * rows_here * route_count // experts)
    pair_hot = one_hot.reshape(rows_here * route_count, experts).astype(jnp.int32)
    counts_before = jnp.cumsum(pair_hot, axis=0) - pair_hot
    slot_index = jnp.sum(counts_before * pair_hot, axis=1)
    target = expert_routes.reshape(-1) * capacity + slot_index
    placement = target[:, None] == jnp.arange(experts * capacity)[None, :]
    repeated = jnp.repeat(expert_input, route_count, axis=0)
    outgoing = jnp.einsum(
        "pc,pd->cd", placement.astype(jnp.bfloat16), repeated, preferred_element_type=jnp.float32
    )
    outgoing = outgoing.astype(jnp.bfloat16).reshape(experts, capacity, model_width)
    results = expert_block(
        lax.all_to_all(outgoing, "req", split_axis=0, concat_axis=0, tiled=True),
        expand_weight[0],
        expand_bias[0],
        reduce_weight[0],
    )
    share_width = model_width // lax.axis_size("mdl")
    offset = lax.axis_index("mdl") * share_width
    shares = lax.psum_scatter(
        results.astype(jnp.bfloat16), "mdl", scatter_dimension=2, tiled=True
    ).astype(jnp.float32)
    returned = lax.all_to_all(
        shares.astype(jnp.bfloat16), "req", split_axis=0, concat_axis=0, tiled=True
    ).astype(shares.dtype)
    picked = returned.reshape(-1, share_width)[target]
    blended = jnp.sum(
        picked.reshape(rows_here, route_count, share_width) * gate_weights[:, :, None], axis=1
    )
    bias_rows = lax.dynamic_slice_in_dim(reduce_bias, offset, share_width, 1)
    bias_term = jnp.sum(bias_rows[expert_routes] * gate_weights[:, :, None], axis=1)
    residual_share = lax.dynamic_slice_in_dim(residual, offset, share_width, 1).astype(jnp.float32)
    return (residual_share + blended + bias_term).astype(jnp.bfloat16)


def solution(mesh):
    in_specs = (
        P("req", None),
        P("req"),
        P("req", None),
        P("req", None, "mdl"),
        P(),
        P("req", "mdl"),
        P("mdl"),
        P("mdl"),
        P("mdl", "req"),
        P(),
        P(),
        P(),
        P(),
        P("req", None),
        P("req", None, "mdl"),
        P("req", "mdl"),
        P("req", "mdl", None),
        P(),
    )
    out_specs = P("req", "mdl")
    return jax.shard_map(shards, mesh=mesh, in_specs=in_specs, out_specs=out_specs, check_vma=False)
```

profile of v0, /device:TPU:32, one launch (start us, length us, event | category | flops | bytes accessed | tf_op | source)
XLA Modules:
  0.0 452.2 jit_solution(11918151416933086248)
XLA Ops:
  6.5 0.7 all-gather.7.cloned.1.call-update
  9.9 0.8 scatter_custom_fusion
  10.9 1.4 fusion.56
  12.9 1.3 gather_fusion.1
  14.9 16.5 %while.1 = (s32[]{:T(128)}, s32[32,16]{0,1:T(8,128)S(1)}, s32[8,2]{0,1:T(2,128)S(1)}, s32[8,14]{1,0:T(8,128)S(1)}, s32[]{:T(128)}, /*index=5*/s32[]{:T(128)}) while((s32[]{:T(128)}, s32[32,16]{0,1:T(8,128)S(1)}, s32[8,2]{0,1:T(2,128)S(1)}, s32[8,14]{1,0:T(8,128)S(1)}, s32[]{:T(128)}, /*index=5*/s32[]{:T(128)}) %tuple.28), condition=%wide.while_cond, body=%wide.while_body.sunk | while | flops 2 | bytes 449 | solution.py:86
  15.5 1.3 dynamic-slice.7
  17.6 1.3 dynamic-slice.7
  19.6 1.3 dynamic-slice.7
  21.7 1.3 dynamic-slice.7
  23.8 1.3 dynamic-slice.7
  25.8 1.3 dynamic-slice.7
  27.9 1.3 dynamic-slice.7
  30.0 1.3 dynamic-slice.7
  31.5 4.8 %gather_fusion = bf16[64,128,128]{2,1,0:T(8,128)(2,1)} fusion(bf16[176,128,128]{2,1,0:T(8,128)(2,1)} %param.21, s32[1024]{0:T(1024)S(1)} %pad_clamp_fusion.4), kind=kCustom, calls=%fused_computation | custom fusion | bytes 4194560 | tf_op jit(solution)/shard_map/gather | solution.py:58
  36.3 5.7 %gather_fusion.3 = bf16[112,128,128]{2,1,0:T(8,128)(2,1)} fusion(bf16[176,128,128]{2,1,0:T(8,128)(2,1)} %param.21, s32[1024]{0:T(1024)S(1)} %pad_clamp_fusion.2), kind=kCustom, calls=%fused_computation.3 | custom fusion | bytes 7340480 | tf_op jit(solution)/shard_map/gather | solution.py:58
  43.8 47.9 %all-gather.7.cloned.1.call-done = bf16[32,90,512]{2,1,0:T(8,128)(2,1)} async-done(((bf16[1,90,512]{2,1,0:T(8,128)(2,1)}), bf16[32,90,512]{2,1,0:T(8,128)(2,1)}) %all-gather.7.cloned.1.call-update) | async-done | bytes 2949136 | tf_op jit(solution)/shard_map/all_gather | solution.py:165
  91.7 4.4 reshape.625
  96.1 76.7 %all-gather.5.cloned.1.call-done = bf16[32,90,640]{2,1,0:T(8,128)(2,1)} async-done(((bf16[1,90,640]{2,1,0:T(8,128)(2,1)}), bf16[32,90,640]{2,1,0:T(8,128)(2,1)}) %all-gather.5.cloned.1.call-update) | async-done | bytes 3686416 | tf_op jit(solution)/shard_map/all_gather | solution.py:164
  172.9 4.9 %reshape.623 = bf16[2880,640]{1,0:T(8,128)(2,1)} reshape(bf16[32,90,640]{2,1,0:T(8,128)(2,1)} %all-gather.5.cloned.1.call-done) | data formatting | bytes 7372800
  177.7 2.8 convolution_add_fusion
  182.2 2.3 fusion.64
  184.6 3.2 fusion.65
  190.6 2.0 fusion.29
  192.7 2.7 fusion.21
  195.4 0.8 scatter_fusion.2
  196.8 3.5 convolution_convert_fusion.2
  200.3 62.1 %all-reduce.3.cloned.1.call-done = bf16[32,2880]{1,0:T(8,128)(2,1)} async-done(((bf16[32,2880]{1,0:T(8,128)(2,1)}), bf16[32,2880]{1,0:T(8,128)(2,1)}) %all-reduce.3.cloned.1.call-update) | async-done | bytes 184336 | tf_op jit(solution)/shard_map/psum | solution.py:197
  262.4 1.1 fusion.12
  263.6 1.1 broadcast_in_dim.57
  264.7 1.6 reshape.490
  266.3 1.8 convolution_convert_fusion.1
  268.1 2.6 copy.49
  270.6 10.1 %all-to-all-start = ((bf16[32,8,2880]{2,1,0:T(8,128)(2,1)}), bf16[32,8,2880]{2,1,0:T(8,128)(2,1)}, u32[]{:S(2)}, u32[]{:S(2)}) async-start(bf16[32,8,2880]{2,1,0:T(8,128)(2,1)} %bitcast.100), calls=%async_computation | async-start | bytes 3014656 | tf_op jit(solution)/shard_map/all_to_all | solution.py:218
  281.0 35.4 %all-to-all-done = bf16[32,8,2880]{2,1,0:T(8,128)(2,1)} async-done(((bf16[32,8,2880]{2,1,0:T(8,128)(2,1)}), bf16[32,8,2880]{2,1,0:T(8,128)(2,1)}, u32[]{:S(2)}, u32[]{:S(2)}) %all-to-all-start) | async-done | bytes 1474592 | tf_op jit(solution)/shard_map/all_to_all | solution.py:218
  316.4 4.9 %fusion.5 = f32[256,720]{0,1:T(8,128)} fusion(bf16[1,2880,720]{1,2,0:T(8,128)(2,1)} %param.32, bf16[32,8,2880]{2,1,0:T(8,128)(2,1)} %all-to-all-done, f32[720]{0:T(1024)S(1)} %reduce.1), kind=kOutput, calls=%fused_computation.22 | convolution fusion | flops 1061867520 | bytes 6361920 | tf_op jit(solution)/shard_map/dot_general | solution.py:129
  321.3 2.1 slice.39
  323.4 2.1 slice.40
  325.8 2.1 convolution_convert_fusion
  327.8 20.3 %copy.58 = bf16[32,8,2880]{1,0,2:T(8,128)(2,1)} copy(bf16[32,8,2880]{2,1,0:T(8,128)(2,1)} %convolution_convert_fusion) | data formatting | bytes 2949120
  348.2 32.7 %reshape.631 = bf16[2880,256]{1,0:T(8,128)(2,1)} reshape(bf16[2880,32,8]{2,1,0:T(8,128)(2,1)} %bitcast.94) | data formatting | bytes 2949120
  381.4 0.9 constant_dynamic-slice_fusion.1
  382.3 0.8 gather_fusion.7
  383.4 30.0 %reduce-scatter.4.cloned.1.call-done = bf16[360,256]{1,0:T(8,128)(2,1)} async-done(((bf16[2880,256]{1,0:T(8,128)(2,1)}), bf16[360,256]{1,0:T(8,128)(2,1)}) %reduce-scatter.4.cloned.1.call-update) | async-done | bytes 184336
  413.4 5.4 %reshape.632 = bf16[360,32,8]{2,1,0:T(8,128)(2,1)} reshape(bf16[360,256]{1,0:T(8,128)(2,1)} %reduce-scatter.4.cloned.1.call-done) | data formatting | bytes 368640
  418.8 4.5 copy.59
  423.3 10.0 %all-to-all-start.1 = ((bf16[32,8,360]{2,1,0:T(8,128)(2,1)}), bf16[32,8,360]{2,1,0:T(8,128)(2,1)S(1)}, u32[]{:S(2)}, u32[]{:S(2)}) async-start(bf16[32,8,360]{2,1,0:T(8,128)(2,1)} %copy.59), calls=%async_computation.1 | async-start | bytes 393216 | tf_op jit(solution)/shard_map/all_to_all | solution.py:228
  433.6 10.2 %all-to-all-done.1 = bf16[32,8,360]{2,1,0:T(8,128)(2,1)S(1)} async-done(((bf16[32,8,360]{2,1,0:T(8,128)(2,1)}), bf16[32,8,360]{2,1,0:T(8,128)(2,1)S(1)}, u32[]{:S(2)}, u32[]{:S(2)}) %all-to-all-start.1) | async-done | bytes 184352 | tf_op jit(solution)/shard_map/all_to_all | solution.py:228
  443.8 0.8 gather_fusion.6
  (148 shorter events, 19.8 us)
Async XLA Ops:
  6.5 319.2 %copy-start = (bf16[1,360,2880]{2,1,0:T(8,128)(2,1)S(1)}, bf16[1,360,2880]{2,1,0:T(8,128)(2,1)}, u32[]{:S(2)}) copy-start(bf16[1,360,2880]{2,1,0:T(8,128)(2,1)} %param.34) | copy-start | bytes 6220804
  6.5 85.2 %all-gather.7.cloned.1.call-start = ((), (), s32[]{:S(2)}) async-start(), calls=%async_computation.5 | async-start | bytes 3244032 | tf_op jit(solution)/shard_map/all_gather | solution.py:165
  7.3 165.6 %all-gather.5.cloned.1.call-start = ((), (), s32[]{:S(2)}) async-start(), calls=%async_computation.4 | async-start | bytes 4055040 | tf_op jit(solution)/shard_map/all_gather | solution.py:164
  8.0 254.4 %all-reduce.3.cloned.1.call-start = ((), (), s32[]{:S(2)}) async-start(), calls=%async_computation.3 | async-start | bytes 376832 | tf_op jit(solution)/shard_map/psum | solution.py:197
  36.3 5.7 %copy-start.5 = (s32[32,4]{0,1:T(4,128)S(1)}, s32[32,4]{0,1:T(4,128)}, u32[]{:S(2)}) copy-start(s32[32,4]{0,1:T(4,128)} %param.31) | copy-start | bytes 1540
  36.3 6.4 %copy-start.3 = (bf16[32,2880]{1,0:T(8,128)(2,1)S(1)}, bf16[32,2880]{1,0:T(8,128)(2,1)}, u32[]{:S(2)}) copy-start(bf16[32,2880]{1,0:T(8,128)(2,1)} %param.18) | copy-start | bytes 552964
  36.3 7.2 %copy-start.2 = (s32[32]{0:T(128)S(1)}, s32[32]{0:T(128)}, u32[]{:S(2)}) copy-start(s32[32]{0:T(128)} %param.19) | copy-start | bytes 388
  96.1 81.6 %copy-start.8 = (f32[2880]{0:T(1024)S(1)}, f32[2880]{0:T(1024)}, u32[]{:S(2)}) copy-start(f32[2880]{0:T(1024)} %param.22) | copy-start | bytes 34564
  96.1 81.6 %copy-start.9 = (f32[640]{0:T(1024)S(1)}, f32[640]{0:T(1024)}, u32[]{:S(2)}) copy-start(f32[640]{0:T(1024)} %param.24) | copy-start | bytes 7684
  180.6 4.0 copy-start.11
  195.4 67.0 %copy-start.7 = (f32[2880]{0:T(1024)S(1)}, f32[2880]{0:T(1024)}, u32[]{:S(2)}) copy-start(f32[2880]{0:T(1024)} %param.27) | copy-start | bytes 34564
  195.4 68.1 %copy-start.6 = (f32[2880]{0:T(1024)S(1)}, f32[2880]{0:T(1024)}, u32[]{:S(2)}) copy-start(f32[2880]{0:T(1024)} %param.28) | copy-start | bytes 34564
  268.1 12.9 %copy-start.10 = (f32[1,720]{1,0:T(1,128)S(1)}, f32[1,720]{1,0:T(1,128)}, u32[]{:S(2)}) copy-start(f32[1,720]{1,0:T(1,128)} %param.33) | copy-start | bytes 8644
  270.6 45.8 %all-to-all-start = ((bf16[32,8,2880]{2,1,0:T(8,128)(2,1)}), bf16[32,8,2880]{2,1,0:T(8,128)(2,1)}, u32[]{:S(2)}, u32[]{:S(2)}) async-start(bf16[32,8,2880]{2,1,0:T(8,128)(2,1)} %bitcast.100), calls=%async_computation | async-start | bytes 3014656 | tf_op jit(solution)/shard_map/all_to_all | solution.py:218
  280.7 132.7 %reduce-scatter.4.cloned.1.call-start = ((), (), s32[]{:S(2)}) async-start(), calls=%async_computation.6 | async-start | bytes 1658880
  380.9 2.2 copy-start.4
  380.9 2.2 copy-start.12
  418.8 26.9 %copy-start.1 = (bf16[1,360,2880]{2,1,0:T(8,128)(2,1)S(1)}, bf16[1,360,2880]{2,1,0:T(8,128)(2,1)}, u32[]{:S(2)}) copy-start(bf16[1,360,2880]{2,1,0:T(8,128)(2,1)} %param.34) | copy-start | bytes 6220804
  423.3 20.5 %all-to-all-start.1 = ((bf16[32,8,360]{2,1,0:T(8,128)(2,1)}), bf16[32,8,360]{2,1,0:T(8,128)(2,1)S(1)}, u32[]{:S(2)}, u32[]{:S(2)}) async-start(bf16[32,8,360]{2,1,0:T(8,128)(2,1)} %copy.59), calls=%async_computation.1 | async-start | bytes 393216 | tf_op jit(solution)/shard_map/all_to_all | solution.py:228
Sparse Core Ops, SparseCore 0:
  9.9 81.7 all-gather.6
  94.3 78.5 all-gather.4
  200.4 61.9 all-reduce.2
  381.1 32.2 reduce-scatter.3
where the time goes:
time: 454 us; the launch traced here: 452 us
  waiting for transfers between devices  264 us (58%)
  local copies, waits for them, and re-layouts  116 us (26%)
  matrix products  25.9 us (6%)
  starting transfers between devices  20.4 us (4%)
  between operations  13.7 us (3%)
  other arithmetic  12.6 us (3%)
    all_gather x1, waiting for transfers between devices, shards(): lax.all_gather(qkv_weight, 'req', axis=0, tiled=True)  76.7 us
    unnamed x33, local copies, waits for them, and re-layouts  72.4 us
    psum x1, waiting for transfers between devices, shards(): lax.psum(partial_value.astype(jnp.bfloat16), 'mdl').astype(jnp.float32)  62.1 us
    all_gather x1, waiting for transfers between devices, shards(): lax.all_gather(output_weight, 'req', axis=1, tiled=True)  47.9 us
    all_to_all x1, waiting for transfers between devices, shards(): lax.all_to_all(outgoing, 'req', split_axis=0, concat_axis=0, tiled=True)  35.4 us
    unnamed x5, waiting for transfers between devices  31.5 us
    gather x40, local copies, waits for them, and re-layouts  16.5 us
    gather x2, local copies, waits for them, and re-layouts, part_scores(): cache_page_store[table].reshape(row_count, -1, cache_page_store.shape[-1])  10.5 us
  transfers between devices with their start and end apart: 6, of which 6 were waited for; matrix products, arithmetic and copies ran while one was open for 9% of the time, Pallas kernels for 0%

commit v1 on v0

--- a/solution.py
+++ b/solution.py
@@ -161,7 +161,9 @@
     rows_here, model_width = hidden_state.shape
     normed = normalize(hidden_state, attention_gain).astype(jnp.bfloat16)
     qkv_full, output_full = (
-        lax.all_gather(qkv_weight, "req", axis=0, tiled=True),
+        jnp.concatenate(
+            lax.all_to_all(jnp.stack([qkv_weight] * lax.axis_size("req")), "req", 0, 0), axis=0
+        ),
         lax.all_gather(output_weight, "req", axis=1, tiled=True),
     )
     projected_rows = jnp.dot(normed, qkv_full, preferred_element_type=jnp.float32)

time: 454 us -> 419 us (0.923)
  waiting for transfers between devices: 264 us -> 216 us
  starting transfers between devices: 20.4 us -> 31.8 us
    all_gather x1 -> x0, waiting for transfers between devices: 76.7 us -> none  [shards(): lax.all_gather(qkv_weight, 'req', axis=0, tiled=True)]
    all_gather x1, waiting for transfers between devices: 47.9 us -> 76.1 us  [shards(): lax.all_gather(output_weight, 'req', axis=1, tiled=True)]
    all_to_all x0 -> x1, starting transfers between devices: none -> 11.4 us  [shards(): lax.all_to_all(jnp.stack([qkv_weight] * lax.axis_size('req')), 'req', 0, 0)]
    unnamed x33 -> x32, local copies, waits for them, and re-layouts: 72.4 us -> 67.4 us
    reshape x1 -> x2, local copies, waits for them, and re-layouts: 0.09 us -> 4.97 us  [the longest x1 4.88 us: shards(): jnp.concatenate(lax.all_to_all(jnp.stack([qkv_weight] * lax.axis_size('re...]
    unnamed x5 -> x4, waiting for transfers between devices: 31.5 us -> 30.7 us
  transfers between devices with their start and end apart: 6 -> 6, of which waited for: 6 -> 5; matrix products, arithmetic and copies ran while one was open for 9% -> 10% of each run, Pallas kernels for 0% -> 0%
where the time goes in v1:
time: 419 us; the launch traced here: 417 us
  waiting for transfers between devices  216 us (52%)
  local copies, waits for them, and re-layouts  119 us (28%)
  starting transfers between devices  31.8 us (8%)
  matrix products  25.9 us (6%)
  between operations  13.7 us (3%)
  other arithmetic  10.6 us (3%)
    all_gather x1, waiting for transfers between devices, shards(): lax.all_gather(output_weight, 'req', axis=1, tiled=True)  76.1 us
    unnamed x32, local copies, waits for them, and re-layouts  67.4 us
    psum x1, waiting for transfers between devices, shards(): lax.psum(partial_value.astype(jnp.bfloat16), 'mdl').astype(jnp.float32)  63.7 us
    all_to_all x1, waiting for transfers between devices, shards(): lax.all_to_all(outgoing, 'req', split_axis=0, concat_axis=0, tiled=True)  35.4 us
    unnamed x4, waiting for transfers between devices  30.7 us
    gather x40, local copies, waits for them, and re-layouts  16.8 us
    all_to_all x1, starting transfers between devices, shards(): lax.all_to_all(jnp.stack([qkv_weight] * lax.axis_size('req')), 'req', 0, 0)  11.4 us
    gather x2, local copies, waits for them, and re-layouts, part_scores(): cache_page_store[table].reshape(row_count, -1, cache_page_store.shape[-1])  10.5 us
  transfers between devices with their start and end apart: 6, of which 5 were waited for; matrix products, arithmetic and copies ran while one was open for 10% of the time, Pallas kernels for 0%

profile of v1, /device:TPU:32, one launch (start us, length us, event | category | flops | bytes accessed | tf_op | source)
XLA Modules:
  0.0 416.7 jit_solution(7398898075220866958)
XLA Ops:
  6.5 3.3 stack.2
  9.8 11.4 %all-to-all-start = ((bf16[32,90,640]{2,1,0:T(8,128)(2,1)}), bf16[32,90,640]{2,1,0:T(8,128)(2,1)}, u32[]{:S(2)}, u32[]{:S(2)}) async-start(bf16[32,90,640]{2,1,0:T(8,128)(2,1)} %stack.2), calls=%async_computation | async-start | bytes 7864320 | tf_op jit(solution)/shard_map/all_to_all | solution.py:165
  21.2 0.7 all-gather.3.cloned.1.call-update
  22.5 0.8 scatter_custom_fusion
  26.1 16.9 %while.1 = (s32[]{:T(128)}, s32[32,16]{0,1:T(8,128)S(1)}, s32[8,2]{0,1:T(2,128)S(1)}, s32[8,14]{1,0:T(8,128)S(1)}, s32[]{:T(128)}, /*index=5*/s32[]{:T(128)}) while((s32[]{:T(128)}, s32[32,16]{0,1:T(8,128)S(1)}, s32[8,2]{0,1:T(2,128)S(1)}, s32[8,14]{1,0:T(8,128)S(1)}, s32[]{:T(128)}, /*index=5*/s32[]{:T(128)}) %tuple.28), condition=%wide.while_cond, body=%wide.while_body.sunk | while | flops 2 | bytes 449 | solution.py:86
  26.7 1.3 dynamic-slice.7
  28.8 1.3 dynamic-slice.7
  30.9 1.3 dynamic-slice.7
  33.1 1.3 dynamic-slice.7
  35.2 1.3 dynamic-slice.7
  37.3 1.3 dynamic-slice.7
  39.4 1.3 dynamic-slice.7
  41.5 1.3 dynamic-slice.7
  43.0 4.8 %gather_fusion = bf16[64,128,128]{2,1,0:T(8,128)(2,1)} fusion(bf16[176,128,128]{2,1,0:T(8,128)(2,1)} %param.21, s32[1024]{0:T(1024)S(1)} %pad_clamp_fusion.4), kind=kCustom, calls=%fused_computation | custom fusion | bytes 4194560 | tf_op jit(solution)/shard_map/gather | solution.py:58
  47.9 5.7 %gather_fusion.3 = bf16[112,128,128]{2,1,0:T(8,128)(2,1)} fusion(bf16[176,128,128]{2,1,0:T(8,128)(2,1)} %param.21, s32[1024]{0:T(1024)S(1)} %pad_clamp_fusion.2), kind=kCustom, calls=%fused_computation.3 | custom fusion | bytes 7340480 | tf_op jit(solution)/shard_map/gather | solution.py:58
  55.4 76.1 %all-gather.3.cloned.1.call-done = bf16[32,90,512]{2,1,0:T(8,128)(2,1)} async-done(((bf16[1,90,512]{2,1,0:T(8,128)(2,1)}), bf16[32,90,512]{2,1,0:T(8,128)(2,1)}) %all-gather.3.cloned.1.call-update) | async-done | bytes 2949136 | tf_op jit(solution)/shard_map/all_gather | solution.py:167
  131.5 4.5 %reshape.629 = bf16[2880,512]{1,0:T(8,128)(2,1)} reshape(bf16[32,90,512]{2,1,0:T(8,128)(2,1)} %all-gather.3.cloned.1.call-done) | data formatting | bytes 5898240
  136.0 4.9 %reshape.484 = bf16[2880,640]{1,0:T(8,128)(2,1)} reshape(bf16[32,90,640]{2,1,0:T(8,128)(2,1)} %all-to-all-done) | data formatting | bytes 7372800 | tf_op jit(solution)/shard_map/reshape | solution.py:164
  140.9 2.8 convolution_add_fusion
  145.4 2.3 fusion.64
  147.7 3.2 fusion.65
  153.7 2.0 fusion.29
  155.8 2.7 fusion.21
  158.5 0.8 scatter_fusion.2
  159.9 3.5 convolution_convert_fusion.2
  163.4 63.7 %all-reduce.3.cloned.1.call-done = bf16[32,2880]{1,0:T(8,128)(2,1)} async-done(((bf16[32,2880]{1,0:T(8,128)(2,1)}), bf16[32,2880]{1,0:T(8,128)(2,1)}) %all-reduce.3.cloned.1.call-update) | async-done | bytes 184336 | tf_op jit(solution)/shard_map/psum | solution.py:199
  227.1 1.1 fusion.12
  228.3 1.1 broadcast_in_dim.57
  229.4 1.6 reshape.496
  231.0 1.8 convolution_convert_fusion.1
  232.7 2.6 copy.49
  235.3 10.1 %all-to-all-start.1 = ((bf16[32,8,2880]{2,1,0:T(8,128)(2,1)}), bf16[32,8,2880]{2,1,0:T(8,128)(2,1)}, u32[]{:S(2)}, u32[]{:S(2)}) async-start(bf16[32,8,2880]{2,1,0:T(8,128)(2,1)} %bitcast.99), calls=%async_computation.1 | async-start | bytes 3014656 | tf_op jit(solution)/shard_map/all_to_all | solution.py:220
  245.7 35.4 %all-to-all-done.1 = bf16[32,8,2880]{2,1,0:T(8,128)(2,1)} async-done(((bf16[32,8,2880]{2,1,0:T(8,128)(2,1)}), bf16[32,8,2880]{2,1,0:T(8,128)(2,1)}, u32[]{:S(2)}, u32[]{:S(2)}) %all-to-all-start.1) | async-done | bytes 1474592 | tf_op jit(solution)/shard_map/all_to_all | solution.py:220
  281.1 4.9 %fusion.5 = f32[256,720]{0,1:T(8,128)} fusion(bf16[1,2880,720]{1,2,0:T(8,128)(2,1)} %param.32, bf16[32,8,2880]{2,1,0:T(8,128)(2,1)} %all-to-all-done.1, f32[720]{0:T(1024)S(1)} %reduce.1), kind=kOutput, calls=%fused_computation.22 | convolution fusion | flops 1061867520 | bytes 6361920 | tf_op jit(solution)/shard_map/dot_general | solution.py:129
  286.0 2.1 slice.39
  288.1 2.1 slice.40
  290.5 2.1 convolution_convert_fusion
  292.6 20.3 %copy.58 = bf16[32,8,2880]{1,0,2:T(8,128)(2,1)} copy(bf16[32,8,2880]{2,1,0:T(8,128)(2,1)} %convolution_convert_fusion) | data formatting | bytes 2949120
  312.9 32.7 %reshape.635 = bf16[2880,256]{1,0:T(8,128)(2,1)} reshape(bf16[2880,32,8]{2,1,0:T(8,128)(2,1)} %bitcast.93) | data formatting | bytes 2949120
  346.1 0.9 constant_dynamic-slice_fusion.1
  347.0 0.8 gather_fusion.7
  348.1 30.0 %reduce-scatter.4.cloned.1.call-done = bf16[360,256]{1,0:T(8,128)(2,1)} async-done(((bf16[2880,256]{1,0:T(8,128)(2,1)}), bf16[360,256]{1,0:T(8,128)(2,1)}) %reduce-scatter.4.cloned.1.call-update) | async-done | bytes 184336
  378.1 5.4 %reshape.636 = bf16[360,32,8]{2,1,0:T(8,128)(2,1)} reshape(bf16[360,256]{1,0:T(8,128)(2,1)} %reduce-scatter.4.cloned.1.call-done) | data formatting | bytes 368640
  383.4 4.3 %copy.59 = bf16[32,8,360]{2,1,0:T(8,128)(2,1)} copy(bf16[32,8,360]{1,0,2:T(8,128)(2,1)} %bitcast.98) | data formatting | bytes 368640
  387.8 10.1 %all-to-all-start.2 = ((bf16[32,8,360]{2,1,0:T(8,128)(2,1)}), bf16[32,8,360]{2,1,0:T(8,128)(2,1)S(1)}, u32[]{:S(2)}, u32[]{:S(2)}) async-start(bf16[32,8,360]{2,1,0:T(8,128)(2,1)} %copy.59), calls=%async_computation.2 | async-start | bytes 393216 | tf_op jit(solution)/shard_map/all_to_all | solution.py:230
  398.2 10.2 %all-to-all-done.2 = bf16[32,8,360]{2,1,0:T(8,128)(2,1)S(1)} async-done(((bf16[32,8,360]{2,1,0:T(8,128)(2,1)}), bf16[32,8,360]{2,1,0:T(8,128)(2,1)S(1)}, u32[]{:S(2)}, u32[]{:S(2)}) %all-to-all-start.2) | async-done | bytes 184352 | tf_op jit(solution)/shard_map/all_to_all | solution.py:230
  408.4 0.8 gather_fusion.6
  409.5 0.7 add_convert_fusion.2
  (148 shorter events, 18.5 us)
Async XLA Ops:
  6.5 283.9 %copy-start = (bf16[1,360,2880]{2,1,0:T(8,128)(2,1)S(1)}, bf16[1,360,2880]{2,1,0:T(8,128)(2,1)}, u32[]{:S(2)}) copy-start(bf16[1,360,2880]{2,1,0:T(8,128)(2,1)} %param.34) | copy-start | bytes 6220804
  9.8 12.2 %copy-start.8 = (s32[32,16]{0,1:T(8,128)S(1)}, s32[32,16]{0,1:T(8,128)}, u32[]{:S(2)}) copy-start(s32[32,16]{0,1:T(8,128)} %param.20) | copy-start | bytes 6148
  9.8 12.4 %copy-start.1 = (s32[32]{0:T(128)S(1)}, s32[32]{0:T(128)}, u32[]{:S(2)}) copy-start(s32[32]{0:T(128)} %param.19) | copy-start | bytes 388
  9.8 126.2 %all-to-all-start = ((bf16[32,90,640]{2,1,0:T(8,128)(2,1)}), bf16[32,90,640]{2,1,0:T(8,128)(2,1)}, u32[]{:S(2)}, u32[]{:S(2)}) async-start(bf16[32,90,640]{2,1,0:T(8,128)(2,1)} %stack.2), calls=%async_computation | async-start | bytes 7864320 | tf_op jit(solution)/shard_map/all_to_all | solution.py:165
  21.2 110.3 %all-gather.3.cloned.1.call-start = ((), (), s32[]{:S(2)}) async-start(), calls=%async_computation.5 | async-start | bytes 3244032 | tf_op jit(solution)/shard_map/all_gather | solution.py:167
  21.9 205.2 %all-reduce.3.cloned.1.call-start = ((), (), s32[]{:S(2)}) async-start(), calls=%async_computation.4 | async-start | bytes 376832 | tf_op jit(solution)/shard_map/psum | solution.py:199
  47.9 5.7 %copy-start.4 = (s32[32,4]{0,1:T(4,128)S(1)}, s32[32,4]{0,1:T(4,128)}, u32[]{:S(2)}) copy-start(s32[32,4]{0,1:T(4,128)} %param.31) | copy-start | bytes 1540
  47.9 6.4 %copy-start.2 = (bf16[32,2880]{1,0:T(8,128)(2,1)S(1)}, bf16[32,2880]{1,0:T(8,128)(2,1)}, u32[]{:S(2)}) copy-start(bf16[32,2880]{1,0:T(8,128)(2,1)} %param.18) | copy-start | bytes 552964
  136.0 4.9 %copy-start.7 = (f32[2880]{0:T(1024)S(1)}, f32[2880]{0:T(1024)}, u32[]{:S(2)}) copy-start(f32[2880]{0:T(1024)} %param.22) | copy-start | bytes 34564
  136.0 4.9 %copy-start.9 = (f32[640]{0:T(1024)S(1)}, f32[640]{0:T(1024)}, u32[]{:S(2)}) copy-start(f32[640]{0:T(1024)} %param.24) | copy-start | bytes 7684
  143.7 4.0 copy-start.11
  158.5 68.6 %copy-start.6 = (f32[2880]{0:T(1024)S(1)}, f32[2880]{0:T(1024)}, u32[]{:S(2)}) copy-start(f32[2880]{0:T(1024)} %param.27) | copy-start | bytes 34564
  158.5 69.7 %copy-start.5 = (f32[2880]{0:T(1024)S(1)}, f32[2880]{0:T(1024)}, u32[]{:S(2)}) copy-start(f32[2880]{0:T(1024)} %param.28) | copy-start | bytes 34564
  232.7 12.9 %copy-start.10 = (f32[1,720]{1,0:T(1,128)S(1)}, f32[1,720]{1,0:T(1,128)}, u32[]{:S(2)}) copy-start(f32[1,720]{1,0:T(1,128)} %param.33) | copy-start | bytes 8644
  235.3 45.8 %all-to-all-start.1 = ((bf16[32,8,2880]{2,1,0:T(8,128)(2,1)}), bf16[32,8,2880]{2,1,0:T(8,128)(2,1)}, u32[]{:S(2)}, u32[]{:S(2)}) async-start(bf16[32,8,2880]{2,1,0:T(8,128)(2,1)} %bitcast.99), calls=%async_computation.1 | async-start | bytes 3014656 | tf_op jit(solution)/shard_map/all_to_all | solution.py:220
  245.4 132.7 %reduce-scatter.4.cloned.1.call-start = ((), (), s32[]{:S(2)}) async-start(), calls=%async_computation.6 | async-start | bytes 1658880
  345.6 2.2 copy-start.3
  345.6 2.2 copy-start.12
  387.8 20.6 %all-to-all-start.2 = ((bf16[32,8,360]{2,1,0:T(8,128)(2,1)}), bf16[32,8,360]{2,1,0:T(8,128)(2,1)S(1)}, u32[]{:S(2)}, u32[]{:S(2)}) async-start(bf16[32,8,360]{2,1,0:T(8,128)(2,1)} %copy.59), calls=%async_computation.2 | async-start | bytes 393216 | tf_op jit(solution)/shard_map/all_to_all | solution.py:230
Sparse Core Ops, SparseCore 0:
  24.6 106.8 all-gather.2
  163.5 63.5 all-reduce.2
  345.8 32.2 reduce-scatter.3
